TPU v7x, 256 devices: a whole 4x4x8 slice. The times are simulated.
256 devices in a mesh: vocab: 32 (over y, z), seq: 8 (over x, core).
Axes of the slice: x: 4, y: 4, z: 8, core: 2. Of those that a mesh axis runs over, the one named last changes fastest.
Arguments:
- hidden: bfloat16 [1024, 3584], P('seq', 'vocab'), may hold values from -16 to 16, as said below
- weight: bfloat16 [256000, 3584], P(('vocab', 'seq')), may hold values from -1 to 1, as said below
- targets: int32 [1024], P('seq'), may hold values from 0 to 255999
- loss_mask: int32 [1024], P('seq'), may hold values from 0 to 1, as said below
Outputs:
- lse: float32 [1024], P('seq')
- token_loss: float32 [1024], P('seq')
- ce_mean: float32 [], replicated
- z_root: float32 [], replicated
Inputs may be any that keep to these rules, and one draw needn't show every extreme that they name: Each token's hidden state, of order one. `weight`: rows of order one over the square root of 3584. `loss_mask`: at least one token is counted.
All inputs are finite; a program needn't handle non-finite values.
Results may differ from a plain program's by a relative error of at most 0.0003.
Values may be sent and summed in bfloat16 or wider, within the bound.
No kernel may reach another device: no remote copies, remote signals or barrier semaphores. Data moves between devices by JAX's collectives and lax.ppermute only.
A program may use at most 64 MiB of HBM per device.

v0:
```python
import jax
import jax.numpy as jnp
from jax import lax
from jax.experimental import pallas as pl
from jax.experimental.pallas import tpu as pltpu
from jax.sharding import Mesh
from jax.sharding import PartitionSpec as P


OFFSETS = (0, 1, 3, 2)
LANES = 128
EXTRA = 16
MASKED = 1e30
VMEM = pl.BlockSpec(memory_space=pltpu.VMEM)
HBM = pl.BlockSpec(memory_space=pltpu.HBM)
SMEM = pl.BlockSpec(memory_space=pltpu.SMEM)
SWAP = [(0, 1), (1, 0)]


def shifted(array, axis, offset):
    size = lax.axis_size(axis)
    return lax.ppermute(array, axis, [((k + offset) % size, k) for k in range(size)])


def around(array, axis):
    return [array] + [shifted(array, axis, offset) for offset in OFFSETS[1:]]


def relayed(array, axis):
    half = array.shape[0] // 2
    up = shifted(array, axis, 1)
    down = shifted(array, axis, 3)
    low, high = shifted(up[:half], axis, 1), shifted(down[half:], axis, 3)
    return [array, up, down, low, high]


def exchanged(array, axis):
    return lax.all_to_all(array, axis, 0, 0, tiled=True)


def load_kernel(first, second, out, sems):
    copies = [
        pltpu.make_async_copy(part, out.at[k], sems.at[k])
        for k, part in enumerate((first, second))
    ]
    for copy in copies:
        copy.start()
    for copy in copies:
        copy.wait()


def half_depth(held, k, second, half):
    return jnp.concatenate(
        [
            held[k, :, (2 * j + second) * half : (2 * j + second + 1) * half]
            for j in range(4)
        ],
        axis=1,
    )


def set_rows(table, place, j, lanes, rows):
    half = rows.shape[0]
    table[pl.ds(pl.multiple_of(place[j] * half, half), half), lanes] = rows


def near_kernel(place, x0, x1, held, out, table):
    for j in range(4):
        for i, block in enumerate((x0, x1)):
            lanes = slice(i * LANES, (i + 1) * LANES)
            set_rows(table, place, j, lanes, block[j])
    for k in range(2):
        out[k] = jnp.dot(
            half_depth(held, k, 0, x0.shape[1]),
            table[...],
            preferred_element_type=jnp.float32,
        )


def far_kernel(place, x2, x3, x4, held, out, table):
    for j in range(4):
        set_rows(table, place, j, slice(0, LANES), x2[j])
        far = x3[j] if j < 2 else x4[j - 2]
        set_rows(table, place, j, slice(LANES, 2 * LANES), far)
    for k in range(2):
        out[k] = jnp.dot(
            half_depth(held, k, 0, x2.shape[1]),
            table[...],
            preferred_element_type=jnp.float32,
        )


def head_kernel(
    place, ints, y0, y1, y2, y3, y4, held, near, far, out, table, logits
):
    half = y0.shape[1]
    for i in range(4):
        lanes = slice(i * LANES, (i + 1) * LANES)
        for j, block in enumerate((y0, y1, y2)):
            set_rows(table, place, j, lanes, block[i])
        set_rows(table, place, 3, lanes, y3[i] if i < 2 else y4[i - 2])
    rows = held.shape[1]
    row = lax.broadcasted_iota(jnp.int32, (rows, 256), 0)
    found = {}
    for k in range(2):
        for side in range(2):
            lanes = slice(side * 256, (side + 1) * 256)
            logits[k, side] = (far if side else near)[k] + jnp.dot(
                half_depth(held, k, 1, half),
                table[:, lanes],
                preferred_element_type=jnp.float32,
            )
            peak = jnp.max(logits[k, side], axis=0, keepdims=True)
            total = jnp.sum(jnp.exp(logits[k, side] - peak), axis=0, keepdims=True)
            digits = [
                jnp.concatenate(
                    [ints[2 * side + h, d : d + 1] for h in range(2)], axis=1
                ).astype(jnp.int32)
                for d in range(3)
            ]
            kept = jnp.concatenate(
                [ints[2 * side + h, 3:4] for h in range(2)], axis=1
            ).astype(jnp.float32)
            wanted = digits[0] + 256 * digits[1] + 65536 * digits[2] - place[4 + k]
            target = jnp.sum(
                jnp.where(row == wanted, logits[k, side], 0.0), axis=0, keepdims=True
            )
            found[k, side] = peak, total, jnp.where(kept > 0.5, target, MASKED)
    message = jnp.zeros((8, LANES), jnp.float32)
    line = lax.broadcasted_iota(jnp.int32, (8, LANES), 0)
    for side in range(2):
        (peak, total, target), (peak2, total2, target2) = found[0, side], found[1, side]
        top = jnp.maximum(peak, peak2)
        total = total * jnp.exp(peak - top) + total2 * jnp.exp(peak2 - top)
        lse = top + jnp.log(total)
        target = target + target2
        for i in range(2):
            at = place[6 + side * 2 + i]
            lanes = slice(i * LANES, (i + 1) * LANES)
            message = jnp.where(line == at, lse[:, lanes], message)
            message = jnp.where(line == 4 + at, target[:, lanes], message)
    for k in range(out.shape[0]):
        out[k] = message


def spread_kernel(block, out):
    for k in range(out.shape[0]):
        out[k] = block[...]


def digits_kernel(targets, mask, out):
    line = lax.broadcasted_iota(jnp.int32, out.shape, 0)
    ids = targets[...]
    both = jnp.zeros(out.shape, jnp.float32)
    for k, row in enumerate([ids & 255, (ids >> 8) & 255, ids >> 16, mask[...]]):
        both = jnp.where(line == k, row.astype(jnp.float32), both)
    out[...] = both.astype(out.dtype)


def joined(parts):
    top, summed = parts[0], parts[0]
    for part in parts[1:]:
        top, summed = jnp.maximum(top, part), summed + part
    total = jnp.exp(parts[0] - top)
    for part in parts[1:]:
        total = total + jnp.exp(part - top)
    line = lax.broadcasted_iota(jnp.int32, summed.shape, 0)
    return jnp.where(line < 4, top + jnp.log(total), summed)


def join_kernel(parts, out):
    message = joined([parts[k] for k in range(parts.shape[0])])
    for k in range(out.shape[0]):
        out[k] = message


def last_kernel(place, parts, lse_out, loss_out, mean_out, root_out):
    line = lax.broadcasted_iota(jnp.int32, (4, LANES), 0)
    sums, rows = [], []
    for c in range(2):
        message = joined([parts[k] for k in range(c, parts.shape[0], 2)])
        lse, target = message[:4], message[4:]
        kept = target < 0.5 * MASKED
        loss = jnp.where(kept, lse - target, 0.0)
        rows.append((lse, loss))
        sums.append((loss, jnp.where(kept, lse * lse, 0.0), jnp.where(kept, 1.0, 0.0)))
    for out, first, second in zip((lse_out, loss_out), *rows):
        both = jnp.where(place[10] == 0, first, second)
        out[...] = jnp.sum(
            jnp.where(line == place[6], both, 0.0), axis=0, keepdims=True
        )
    loss, square, count = (
        jnp.sum(first + second, keepdims=True) for first, second in zip(*sums)
    )
    mean_out[...] = loss / count
    root_out[...] = jnp.sqrt(square / count)


def call(kernel, inputs, specs, out_shape, scratch=(), limit=8):
    single = not isinstance(out_shape, tuple)
    return pl.pallas_call(
        kernel,
        out_shape=out_shape,
        in_specs=specs,
        out_specs=VMEM if single else tuple(VMEM for _ in out_shape),
        scratch_shapes=list(scratch),
        compiler_params=pltpu.CompilerParams(vmem_limit_bytes=limit * 1024 * 1024),
    )(*inputs)


def on_device(hidden, weight, targets, loss_mask):
    rows = weight.shape[0]
    x, y, z, c = (lax.axis_index(name) for name in ("x", "y", "z", "c"))
    n_z = lax.axis_size("z")
    other = lax.ppermute(weight, "c", SWAP)
    block = hidden.T
    ints = call(
        digits_kernel,
        (targets[None], loss_mask[None]),
        [VMEM] * 2,
        jax.ShapeDtypeStruct((EXTRA, LANES), block.dtype),
    )
    mine = call(
        spread_kernel,
        (block,),
        [VMEM],
        jax.ShapeDtypeStruct((n_z, *block.shape), block.dtype),
    )
    mine = exchanged(mine, "z")
    first = mine[: n_z // 2].reshape(-1, LANES)
    second = mine[n_z // 2 :].reshape(-1, LANES)
    half = first.shape[0]
    second = jnp.concatenate([second, ints])
    second, first = around(second, "x"), around(first, "y")
    ints = jnp.stack([part[half:] for part in second])
    first = jnp.stack(first)
    second = jnp.stack([part[:half] for part in second])
    held = call(
        load_kernel,
        [pltpu.with_memory_space_constraint(w, pltpu.HBM) for w in (weight, other)],
        [HBM] * 2,
        pltpu.VMEM((2, *weight.shape), weight.dtype),
        [pltpu.SemaphoreType.DMA((2,))],
    )
    by_x, by_y = relayed(first, "x"), relayed(second, "y")

    index = ((y * n_z + z) * 4 + x) * 2 + c
    place = jnp.stack(
        [(y + offset) % 4 for offset in OFFSETS]
        + [index * rows, (index + 1 - 2 * c) * rows]
        + [(x + offset) % 4 for offset in OFFSETS]
        + [c]
    ).astype(jnp.int32)
    depth = weight.shape[1] // 2
    near, far = (
        call(
            kernel,
            (place, *blocks, held),
            [SMEM] + [VMEM] * (len(blocks) + 1),
            pltpu.VMEM((2, rows, 256), jnp.float32),
            [pltpu.VMEM((depth, 256), jnp.bfloat16)],
            24,
        )
        for kernel, blocks in ((near_kernel, by_x[:2]), (far_kernel, by_x[2:]))
    )
    message = call(
        head_kernel,
        (place, ints, *by_y, held, near, far),
        [SMEM] + [VMEM] * 9,
        jax.ShapeDtypeStruct((16, 8, LANES), jnp.float32),
        [
            pltpu.VMEM((depth, 512), jnp.bfloat16),
            pltpu.VMEM((2, 2, rows, 256), jnp.float32),
        ],
        24,
    )
    message = call(
        join_kernel,
        (exchanged(message, ("y", "x")),),
        [VMEM],
        jax.ShapeDtypeStruct((2 * n_z, 8, LANES), jnp.float32),
    )
    line = jax.ShapeDtypeStruct((1, LANES), jnp.float32)
    one = jax.ShapeDtypeStruct((1, 1), jnp.float32)
    lse, loss, mean, root = call(
        last_kernel,
        (place, exchanged(message, ("z", "c"))),
        [SMEM, VMEM],
        (line, line, one, one),
    )
    return (lse[0], loss[0], mean[0, 0], root[0, 0])


def solution(mesh):
    split = Mesh(mesh.devices.reshape(4, 8, 4, 2), ("y", "z", "x", "c"))
    seq, vocab = ("x", "c"), ("y", "z")
    in_specs = (P(seq, vocab), P(vocab + seq, None), P(seq), P(seq))
    out_specs = (P(seq), P(seq), P(), P())

    return jax.shard_map(
        on_device, mesh=split, in_specs=in_specs, out_specs=out_specs, check_vma=False
    )
```

profile of v0, /device:TPU:1, one launch (start us, length us, event | category | flops | bytes accessed | tf_op | source)
XLA Modules:
  0.0 97.1 jit_solution(237120848212555786)
XLA Ops:
  0.6 3.3 %collective-permute-start.7 = (bf16[1000,3584]{1,0:T(8,128)(2,1)}, bf16[1000,3584]{1,0:T(8,128)(2,1)}, u32[]{:S(2)}, u32[]{:S(2)}) collective-permute-start(bf16[1000,3584]{1,0:T(8,128)(2,1)} %first.1), channel_id=1, source_target_pairs={{0,1},{1,0},{2,3},{3,2},{4,5},{5,4},{6,7},{7,6},{8,9},{9,8},{10,11... | collective-permute-start | bytes 21504008 | tf_op jit(solution)/shard_map/ppermute | solution.py:215
  3.9 0.0 copy-start
  3.9 0.7 copy-done
  4.7 0.7 shard_map.76
  5.4 6.5 %all-to-all-start = ((bf16[8,112,128]{2,1,0:T(8,128)(2,1)}), bf16[8,112,128]{2,1,0:T(8,128)(2,1)S(1)}, u32[]{:S(2)}, u32[]{:S(2)}) async-start(bf16[8,112,128]{2,1,0:T(8,128)(2,1)} %shard_map.76), calls=%async_computation | async-start | bytes 458752 | tf_op jit(solution)/shard_map/all_to_all | solution.py:38
  11.9 0.0 copy-start.1
  11.9 0.7 copy-done.1
  12.5 0.0 copy-start.2
  12.5 0.7 copy-done.2
  13.2 10.3 %all-to-all-done = bf16[8,112,128]{2,1,0:T(8,128)(2,1)S(1)} async-done(((bf16[8,112,128]{2,1,0:T(8,128)(2,1)}), bf16[8,112,128]{2,1,0:T(8,128)(2,1)S(1)}, u32[]{:S(2)}, u32[]{:S(2)}) %all-to-all-start) | async-done | bytes 229408 | tf_op jit(solution)/shard_map/all_to_all | solution.py:38
  23.5 2.8 %collective-permute-start.8 = (bf16[448,128]{1,0:T(8,128)(2,1)S(1)}, bf16[448,128]{1,0:T(8,128)(2,1)S(1)}, u32[]{:S(2)}, u32[]{:S(2)}) collective-permute-start(bf16[448,128]{1,0:T(8,128)(2,1)S(1)} %bitcast.44), channel_id=1, source_target_pairs={{64,0},{128,64},{192,128},{0,192},{65,1},{129,65},{193,129},{1,193... | collective-permute-start | bytes 344072 | tf_op jit(solution)/shard_map/ppermute | solution.py:22
  26.3 0.0 collective-permute-start.9
  26.3 1.6 %collective-permute-start.10 = (bf16[448,128]{1,0:T(8,128)(2,1)S(1)}, bf16[448,128]{1,0:T(8,128)(2,1)S(1)}, u32[]{:S(2)}, u32[]{:S(2)}) collective-permute-start(bf16[448,128]{1,0:T(8,128)(2,1)S(1)} %bitcast.46), channel_id=1, source_target_pairs={{128,0},{192,64},{0,128},{64,192},{129,1},{193,65},{1,129},{65,193... | collective-permute-start | bytes 344072 | tf_op jit(solution)/shard_map/ppermute | solution.py:22
  27.9 2.8 %collective-permute-start.2 = (bf16[464,128]{1,0:T(8,128)(2,1)S(1)}, bf16[464,128]{1,0:T(8,128)(2,1)S(1)}, u32[]{:S(2)}, u32[]{:S(2)}) collective-permute-start(bf16[464,128]{1,0:T(8,128)(2,1)S(1)} %pad_maximum_fusion.2), channel_id=1, source_target_pairs={{4,0},{6,2},{0,4},{2,6},{5,1},{7,3},{1,5},{3,7},{12,8},{14,10},{8,... | collective-permute-start | bytes 356360 | tf_op jit(solution)/shard_map/ppermute | solution.py:22
  30.8 0.0 collective-permute-done.8
  30.8 0.3 collective-permute-start.1
  31.1 3.2 %collective-permute-done.9 = bf16[448,128]{1,0:T(8,128)(2,1)S(1)} collective-permute-done((bf16[448,128]{1,0:T(8,128)(2,1)S(1)}, bf16[448,128]{1,0:T(8,128)(2,1)S(1)}, u32[]{:S(2)}, u32[]{:S(2)}) %collective-permute-start.9) | collective-permute-done | bytes 114720 | tf_op jit(solution)/shard_map/ppermute | solution.py:22
  34.3 2.5 %collective-permute-start = (bf16[464,128]{1,0:T(8,128)(2,1)S(1)}, bf16[464,128]{1,0:T(8,128)(2,1)S(1)}, u32[]{:S(2)}, u32[]{:S(2)}) collective-permute-start(bf16[464,128]{1,0:T(8,128)(2,1)S(1)} %pad_maximum_fusion.2), channel_id=1, source_target_pairs={{2,0},{4,2},{6,4},{0,6},{3,1},{5,3},{7,5},{1,7},{10,8},{12,10},{14... | collective-permute-start | bytes 356360 | tf_op jit(solution)/shard_map/ppermute | solution.py:22
  36.8 0.0 collective-permute-done.10
  36.8 0.1 pad_maximum_fusion.1.x0
  36.9 0.6 collective-permute-start.11
  37.5 0.0 collective-permute-done.2
  37.5 0.9 collective-permute-start.12
  38.4 0.0 collective-permute-done.1
  38.5 0.2 collective-permute-done
  38.7 0.1 pad_maximum_fusion.y0
  38.7 0.1 collective-permute-start.3
  38.8 1.5 %collective-permute-start.4 = (bf16[4,448,128]{2,1,0:T(8,128)(2,1)S(1)}, bf16[4,448,128]{2,1,0:T(8,128)(2,1)S(1)}, u32[]{:S(2)}, u32[]{:S(2)}) collective-permute-start(bf16[4,448,128]{2,1,0:T(8,128)(2,1)S(1)} %pad_maximum_fusion.y0), channel_id=1, source_target_pairs={{192,0},{0,64},{64,128},{128,192},{193,1},{1,65},{65,129},{129,193... | collective-permute-start | bytes 1376264 | tf_op jit(solution)/shard_map/ppermute | solution.py:22
  40.3 0.1 stack.86.place
  40.4 7.8 %collective-permute-done.11.x1 = bf16[4,448,128]{2,1,0:T(8,128)(2,1)S(1)} collective-permute-done((bf16[4,448,128]{2,1,0:T(8,128)(2,1)S(1)}, bf16[4,448,128]{2,1,0:T(8,128)(2,1)S(1)}, u32[]{:S(2)}, u32[]{:S(2)}) %collective-permute-start.11) | collective-permute-done | bytes 458784 | tf_op jit(solution)/shard_map/ppermute | solution.py:22
  48.2 3.4 %collective-permute-start.13 = (bf16[2,448,128]{2,1,0:T(8,128)(2,1)S(1)}, bf16[2,448,128]{2,1,0:T(8,128)(2,1)S(1)}, u32[]{:S(2)}, u32[]{:S(2)}) collective-permute-start(bf16[2,448,128]{2,1,0:T(8,128)(2,1)S(1)} %slice.58), channel_id=1, source_target_pairs={{2,0},{4,2},{6,4},{0,6},{3,1},{5,3},{7,5},{1,7},{10,8},{12,10},{14... | collective-permute-start | bytes 688136 | tf_op jit(solution)/shard_map/ppermute | solution.py:22
  51.6 0.0 collective-permute-done.12.x2
  51.6 0.1 collective-permute-start.14
  51.7 0.0 collective-permute-done.3.y1
  51.7 0.1 collective-permute-start.5
  51.8 0.0 collective-permute-done.4.y2
  51.8 1.7 %collective-permute-start.6 = (bf16[2,448,128]{2,1,0:T(8,128)(2,1)S(1)}, bf16[2,448,128]{2,1,0:T(8,128)(2,1)S(1)}, u32[]{:S(2)}, u32[]{:S(2)}) collective-permute-start(bf16[2,448,128]{2,1,0:T(8,128)(2,1)S(1)} %slice.56), channel_id=1, source_target_pairs={{192,0},{0,64},{64,128},{128,192},{193,1},{1,65},{65,129},{129,193... | collective-permute-start | bytes 688136 | tf_op jit(solution)/shard_map/ppermute | solution.py:22
  53.5 0.0 collective-permute-done.7.second
  53.6 5.1 %shard_map.77.held = bf16[2,1000,3584]{2,1,0:T(8,128)(2,1)S(1)} custom-call(bf16[1000,3584]{1,0:T(8,128)(2,1)} %first.1, bf16[1000,3584]{1,0:T(8,128)(2,1)} %collective-permute-done.7.second), custom_call_target="tpu_custom_call" | custom-call | tf_op jit(solution)/shard_map/pallas_call | solution.py:201
  58.7 2.8 %shard_map.78.near = f32[2,1000,256]{2,1,0:T(8,128)S(1)} custom-call(s32[11]{0:T(128)S(1)} %stack.86.place, bf16[4,448,128]{2,1,0:T(8,128)(2,1)S(1)} %pad_maximum_fusion.1.x0, bf16[4,448,128]{2,1,0:T(8,128)(2,1)S(1)} %collective-permute-done.11.x1, bf16[2,1000,3584]{2,1,0:T(8,128)(2,1)S(1)} %shard_map.77.held), custom_call_target="tpu_custom_call" | custom-call | tf_op jit(solution)/shard_map/pallas_call | solution.py:201
  61.4 0.0 collective-permute-done.13.x3
  61.4 0.0 collective-permute-done.14.x4
  61.5 2.8 %shard_map.79.far = f32[2,1000,256]{2,1,0:T(8,128)S(1)} custom-call(s32[11]{0:T(128)S(1)} %stack.86.place, bf16[4,448,128]{2,1,0:T(8,128)(2,1)S(1)} %collective-permute-done.12.x2, bf16[2,448,128]{2,1,0:T(8,128)(2,1)S(1)} %collective-permute-done.13.x3, bf16[2,448,128]{2,1,0:T(8,128)(2,1)S(1)} %collective-permute-done.14.x4, ...), custom_call_target="tpu_custom_call" | custom-call | tf_op jit(solution)/shard_map/pallas_call | solution.py:201
  64.2 0.0 collective-permute-done.5.y3
  64.2 0.0 collective-permute-done.6.y4
  64.2 5.8 %shard_map.80 = f32[16,8,128]{2,1,0:T(8,128)S(1)} custom-call(s32[11]{0:T(128)S(1)} %stack.86.place, bf16[4,16,128]{2,1,0:T(8,128)(2,1)S(1)} %pad_maximum_fusion.3.ints, bf16[4,448,128]{2,1,0:T(8,128)(2,1)S(1)} %pad_maximum_fusion.y0, bf16[4,448,128]{2,1,0:T(8,128)(2,1)S(1)} %collective-permute-done.3.y1, ...), custom_call_target="tpu_custom_call" | custom-call | tf_op jit(solution)/shard_map/pallas_call | solution.py:201
  70.0 11.3 %all_to_all.15.parts = f32[16,8,128]{2,1,0:T(8,128)S(1)} all-to-all(f32[16,8,128]{2,1,0:T(8,128)S(1)} %shard_map.80), channel_id=1, replica_groups=mesh['y'=4,'z'=8,'x'=4,'c'=2] {'y','x'}, dimensions={0} | all-to-all | bytes 131072 | tf_op jit(solution)/shard_map/all_to_all | solution.py:38
  81.4 14.5 %all_to_all.16.parts = f32[16,8,128]{2,1,0:T(8,128)S(1)} all-to-all(f32[16,8,128]{2,1,0:T(8,128)S(1)} %shard_map.81), channel_id=1, replica_groups=mesh['y'=4,'z'=8,'x'=4,'c'=2] {'z','c'}, dimensions={0} | all-to-all | bytes 131072 | tf_op jit(solution)/shard_map/all_to_all | solution.py:38
  95.9 1.2 %shard_map.82 = (f32[1,128]{1,0:T(1,128)}, f32[1,128]{1,0:T(1,128)}, f32[1,1]{1,0:T(1,128)}, f32[1,1]{1,0:T(1,128)}) custom-call(s32[11]{0:T(128)S(1)} %stack.86.place, f32[16,8,128]{2,1,0:T(8,128)S(1)} %all_to_all.16.parts), custom_call_target="tpu_custom_call" | custom-call | tf_op jit(solution)/shard_map/pallas_call | solution.py:201
  (15 shorter events, 0.2 us)
Async XLA Ops:
  0.6 52.9 %collective-permute-start.7 = (bf16[1000,3584]{1,0:T(8,128)(2,1)}, bf16[1000,3584]{1,0:T(8,128)(2,1)}, u32[]{:S(2)}, u32[]{:S(2)}) collective-permute-start(bf16[1000,3584]{1,0:T(8,128)(2,1)} %first.1), channel_id=1, source_target_pairs={{0,1},{1,0},{2,3},{3,2},{4,5},{5,4},{6,7},{7,6},{8,9},{9,8},{10,11... | collective-permute-start | bytes 21504008 | tf_op jit(solution)/shard_map/ppermute | solution.py:215
  3.9 0.7 copy-start
  5.4 18.1 %all-to-all-start = ((bf16[8,112,128]{2,1,0:T(8,128)(2,1)}), bf16[8,112,128]{2,1,0:T(8,128)(2,1)S(1)}, u32[]{:S(2)}, u32[]{:S(2)}) async-start(bf16[8,112,128]{2,1,0:T(8,128)(2,1)} %shard_map.76), calls=%async_computation | async-start | bytes 458752 | tf_op jit(solution)/shard_map/all_to_all | solution.py:38
  11.9 0.7 copy-start.1
  12.5 0.7 copy-start.2
  23.5 7.3 %collective-permute-start.8 = (bf16[448,128]{1,0:T(8,128)(2,1)S(1)}, bf16[448,128]{1,0:T(8,128)(2,1)S(1)}, u32[]{:S(2)}, u32[]{:S(2)}) collective-permute-start(bf16[448,128]{1,0:T(8,128)(2,1)S(1)} %bitcast.44), channel_id=1, source_target_pairs={{64,0},{128,64},{192,128},{0,192},{65,1},{129,65},{193,129},{1,193... | collective-permute-start | bytes 344072 | tf_op jit(solution)/shard_map/ppermute | solution.py:22
  26.3 8.0 %collective-permute-start.9 = (bf16[448,128]{1,0:T(8,128)(2,1)S(1)}, bf16[448,128]{1,0:T(8,128)(2,1)S(1)}, u32[]{:S(2)}, u32[]{:S(2)}) collective-permute-start(bf16[448,128]{1,0:T(8,128)(2,1)S(1)} %bitcast.45), channel_id=1, source_target_pairs={{192,0},{0,64},{64,128},{128,192},{193,1},{1,65},{65,129},{129,193... | collective-permute-start | bytes 344072 | tf_op jit(solution)/shard_map/ppermute | solution.py:22
  26.3 10.5 %collective-permute-start.10 = (bf16[448,128]{1,0:T(8,128)(2,1)S(1)}, bf16[448,128]{1,0:T(8,128)(2,1)S(1)}, u32[]{:S(2)}, u32[]{:S(2)}) collective-permute-start(bf16[448,128]{1,0:T(8,128)(2,1)S(1)} %bitcast.46), channel_id=1, source_target_pairs={{128,0},{192,64},{0,128},{64,192},{129,1},{193,65},{1,129},{65,193... | collective-permute-start | bytes 344072 | tf_op jit(solution)/shard_map/ppermute | solution.py:22
  27.9 9.6 %collective-permute-start.2 = (bf16[464,128]{1,0:T(8,128)(2,1)S(1)}, bf16[464,128]{1,0:T(8,128)(2,1)S(1)}, u32[]{:S(2)}, u32[]{:S(2)}) collective-permute-start(bf16[464,128]{1,0:T(8,128)(2,1)S(1)} %pad_maximum_fusion.2), channel_id=1, source_target_pairs={{4,0},{6,2},{0,4},{2,6},{5,1},{7,3},{1,5},{3,7},{12,8},{14,10},{8,... | collective-permute-start | bytes 356360 | tf_op jit(solution)/shard_map/ppermute | solution.py:22
  30.8 7.7 %collective-permute-start.1 = (bf16[464,128]{1,0:T(8,128)(2,1)S(1)}, bf16[464,128]{1,0:T(8,128)(2,1)S(1)}, u32[]{:S(2)}, u32[]{:S(2)}) collective-permute-start(bf16[464,128]{1,0:T(8,128)(2,1)S(1)} %pad_maximum_fusion.2), channel_id=1, source_target_pairs={{6,0},{0,2},{2,4},{4,6},{7,1},{1,3},{3,5},{5,7},{14,8},{8,10},{10,... | collective-permute-start | bytes 356360 | tf_op jit(solution)/shard_map/ppermute | solution.py:22
  34.3 4.3 %collective-permute-start = (bf16[464,128]{1,0:T(8,128)(2,1)S(1)}, bf16[464,128]{1,0:T(8,128)(2,1)S(1)}, u32[]{:S(2)}, u32[]{:S(2)}) collective-permute-start(bf16[464,128]{1,0:T(8,128)(2,1)S(1)} %pad_maximum_fusion.2), channel_id=1, source_target_pairs={{2,0},{4,2},{6,4},{0,6},{3,1},{5,3},{7,5},{1,7},{10,8},{12,10},{14... | collective-permute-start | bytes 356360 | tf_op jit(solution)/shard_map/ppermute | solution.py:22
  36.9 11.3 %collective-permute-start.11 = (bf16[4,448,128]{2,1,0:T(8,128)(2,1)S(1)}, bf16[4,448,128]{2,1,0:T(8,128)(2,1)S(1)}, u32[]{:S(2)}, u32[]{:S(2)}) collective-permute-start(bf16[4,448,128]{2,1,0:T(8,128)(2,1)S(1)} %pad_maximum_fusion.1.x0), channel_id=1, source_target_pairs={{2,0},{4,2},{6,4},{0,6},{3,1},{5,3},{7,5},{1,7},{10,8},{12,10},{14... | collective-permute-start | bytes 1376264 | tf_op jit(solution)/shard_map/ppermute | solution.py:22
  37.5 14.1 %collective-permute-start.12 = (bf16[4,448,128]{2,1,0:T(8,128)(2,1)S(1)}, bf16[4,448,128]{2,1,0:T(8,128)(2,1)S(1)}, u32[]{:S(2)}, u32[]{:S(2)}) collective-permute-start(bf16[4,448,128]{2,1,0:T(8,128)(2,1)S(1)} %pad_maximum_fusion.1.x0), channel_id=1, source_target_pairs={{6,0},{0,2},{2,4},{4,6},{7,1},{1,3},{3,5},{5,7},{14,8},{8,10},{10,... | collective-permute-start | bytes 1376264 | tf_op jit(solution)/shard_map/ppermute | solution.py:22
  38.7 12.9 %collective-permute-start.3 = (bf16[4,448,128]{2,1,0:T(8,128)(2,1)S(1)}, bf16[4,448,128]{2,1,0:T(8,128)(2,1)S(1)}, u32[]{:S(2)}, u32[]{:S(2)}) collective-permute-start(bf16[4,448,128]{2,1,0:T(8,128)(2,1)S(1)} %pad_maximum_fusion.y0), channel_id=1, source_target_pairs={{64,0},{128,64},{192,128},{0,192},{65,1},{129,65},{193,129},{1,193... | collective-permute-start | bytes 1376264 | tf_op jit(solution)/shard_map/ppermute | solution.py:22
  38.8 13.0 %collective-permute-start.4 = (bf16[4,448,128]{2,1,0:T(8,128)(2,1)S(1)}, bf16[4,448,128]{2,1,0:T(8,128)(2,1)S(1)}, u32[]{:S(2)}, u32[]{:S(2)}) collective-permute-start(bf16[4,448,128]{2,1,0:T(8,128)(2,1)S(1)} %pad_maximum_fusion.y0), channel_id=1, source_target_pairs={{192,0},{0,64},{64,128},{128,192},{193,1},{1,65},{65,129},{129,193... | collective-permute-start | bytes 1376264 | tf_op jit(solution)/shard_map/ppermute | solution.py:22
  48.2 13.3 %collective-permute-start.13 = (bf16[2,448,128]{2,1,0:T(8,128)(2,1)S(1)}, bf16[2,448,128]{2,1,0:T(8,128)(2,1)S(1)}, u32[]{:S(2)}, u32[]{:S(2)}) collective-permute-start(bf16[2,448,128]{2,1,0:T(8,128)(2,1)S(1)} %slice.58), channel_id=1, source_target_pairs={{2,0},{4,2},{6,4},{0,6},{3,1},{5,3},{7,5},{1,7},{10,8},{12,10},{14... | collective-permute-start | bytes 688136 | tf_op jit(solution)/shard_map/ppermute | solution.py:22
  51.6 9.9 %collective-permute-start.14 = (bf16[2,448,128]{2,1,0:T(8,128)(2,1)S(1)}, bf16[2,448,128]{2,1,0:T(8,128)(2,1)S(1)}, u32[]{:S(2)}, u32[]{:S(2)}) collective-permute-start(bf16[2,448,128]{2,1,0:T(8,128)(2,1)S(1)} %slice.59), channel_id=1, source_target_pairs={{6,0},{0,2},{2,4},{4,6},{7,1},{1,3},{3,5},{5,7},{14,8},{8,10},{10,... | collective-permute-start | bytes 688136 | tf_op jit(solution)/shard_map/ppermute | solution.py:22
  51.7 12.5 %collective-permute-start.5 = (bf16[2,448,128]{2,1,0:T(8,128)(2,1)S(1)}, bf16[2,448,128]{2,1,0:T(8,128)(2,1)S(1)}, u32[]{:S(2)}, u32[]{:S(2)}) collective-permute-start(bf16[2,448,128]{2,1,0:T(8,128)(2,1)S(1)} %slice.55), channel_id=1, source_target_pairs={{64,0},{128,64},{192,128},{0,192},{65,1},{129,65},{193,129},{1,193... | collective-permute-start | bytes 688136 | tf_op jit(solution)/shard_map/ppermute | solution.py:22
  51.8 12.4 %collective-permute-start.6 = (bf16[2,448,128]{2,1,0:T(8,128)(2,1)S(1)}, bf16[2,448,128]{2,1,0:T(8,128)(2,1)S(1)}, u32[]{:S(2)}, u32[]{:S(2)}) collective-permute-start(bf16[2,448,128]{2,1,0:T(8,128)(2,1)S(1)} %slice.56), channel_id=1, source_target_pairs={{192,0},{0,64},{64,128},{128,192},{193,1},{1,65},{65,129},{129,193... | collective-permute-start | bytes 688136 | tf_op jit(solution)/shard_map/ppermute | solution.py:22
where the time goes:
time: 97.5 us; the launch traced here: 97.1 us
  starting transfers between devices  28.2 us (29%)
  blocking collectives  25.8 us (26%)
  waiting for transfers between devices  21.5 us (22%)
  Pallas kernels  18.4 us (19%)
  local copies, waits for them, and re-layouts  2.25 us (2%)
    all_to_all x2, blocking collectives, exchanged(): return lax.all_to_all(array, axis, 0, 0, tiled=True)  25.8 us
    ppermute x14, starting transfers between devices, shifted(): lax.ppermute(array, axis, [((k + offset) % size, k) for k in range(size)])  18.4 us
    pallas_call x8, Pallas kernels, call(): pl.pallas_call(kernel, out_shape=out_shape, in_specs=specs, out_specs=VME...  18.4 us
    ppermute x14, waiting for transfers between devices, shifted(): lax.ppermute(array, axis, [((k + offset) % size, k) for k in range(size)])  11.2 us
    all_to_all x1, waiting for transfers between devices, exchanged(): return lax.all_to_all(array, axis, 0, 0, tiled=True)  10.3 us
    all_to_all x1, starting transfers between devices, exchanged(): return lax.all_to_all(array, axis, 0, 0, tiled=True)  6.48 us
    ppermute x1, starting transfers between devices, on_device(): other = lax.ppermute(weight, 'c', SWAP)  3.29 us
    unnamed x6, local copies, waits for them, and re-layouts  2.05 us
  transfers between devices with their start and end apart: 16, of which 4 were waited for; matrix products, arithmetic and copies ran while one was open for 0% of the time, Pallas kernels for 12%

commit v1 on v0

--- a/solution.py
+++ b/solution.py
@@ -39,8 +39,14 @@
 
 
 def load_kernel(first, second, out, sems):
+    chunk = first.shape[0] // sems.shape[1]
     copies = [
-        pltpu.make_async_copy(part, out.at[k], sems.at[k])
+        pltpu.make_async_copy(
+            part.at[pl.ds(n * chunk, chunk)],
+            out.at[k, pl.ds(n * chunk, chunk)],
+            sems.at[k, n],
+        )
+        for n in range(sems.shape[1])
         for k, part in enumerate((first, second))
     ]
     for copy in copies:
@@ -240,7 +246,7 @@
         [pltpu.with_memory_space_constraint(w, pltpu.HBM) for w in (weight, other)],
         [HBM] * 2,
         pltpu.VMEM((2, *weight.shape), weight.dtype),
-        [pltpu.SemaphoreType.DMA((2,))],
+        [pltpu.SemaphoreType.DMA((2, 5))],
     )
     by_x, by_y = relayed(first, "x"), relayed(second, "y")
 

time: 97.5 us -> 97.6 us (level)
  no operation moved by 1% of the time
where the time goes in v1:
time: 97.6 us; the launch traced here: 97.2 us
  starting transfers between devices  28.2 us (29%)
  blocking collectives  25.8 us (26%)
  waiting for transfers between devices  21.5 us (22%)
  Pallas kernels  18.5 us (19%)
  local copies, waits for them, and re-layouts  2.25 us (2%)
    all_to_all x2, blocking collectives, exchanged(): return lax.all_to_all(array, axis, 0, 0, tiled=True)  25.8 us
    pallas_call x8, Pallas kernels, call(): pl.pallas_call(kernel, out_shape=out_shape, in_specs=specs, out_specs=VME...  18.5 us
    ppermute x14, starting transfers between devices, shifted(): lax.ppermute(array, axis, [((k + offset) % size, k) for k in range(size)])  18.4 us
    ppermute x14, waiting for transfers between devices, shifted(): lax.ppermute(array, axis, [((k + offset) % size, k) for k in range(size)])  11.2 us
    all_to_all x1, waiting for transfers between devices, exchanged(): return lax.all_to_all(array, axis, 0, 0, tiled=True)  10.3 us
    all_to_all x1, starting transfers between devices, exchanged(): return lax.all_to_all(array, axis, 0, 0, tiled=True)  6.48 us
    ppermute x1, starting transfers between devices, on_device(): other = lax.ppermute(weight, 'c', SWAP)  3.29 us
    unnamed x6, local copies, waits for them, and re-layouts  2.05 us
  transfers between devices with their start and end apart: 16, of which 4 were waited for; matrix products, arithmetic and copies ran while one was open for 0% of the time, Pallas kernels for 12%

profile of v1, /device:TPU:1, one launch (start us, length us, event | category | flops | bytes accessed | tf_op | source)
XLA Modules:
  0.0 97.2 jit_solution(4729636561942903149)
XLA Ops:
  0.6 3.3 %collective-permute-start.7 = (bf16[1000,3584]{1,0:T(8,128)(2,1)}, bf16[1000,3584]{1,0:T(8,128)(2,1)}, u32[]{:S(2)}, u32[]{:S(2)}) collective-permute-start(bf16[1000,3584]{1,0:T(8,128)(2,1)} %first.1), channel_id=1, source_target_pairs={{0,1},{1,0},{2,3},{3,2},{4,5},{5,4},{6,7},{7,6},{8,9},{9,8},{10,11... | collective-permute-start | bytes 21504008 | tf_op jit(solution)/shard_map/ppermute | solution.py:221
  3.9 0.0 copy-start
  3.9 0.7 copy-done
  4.7 0.7 shard_map.76
  5.4 6.5 %all-to-all-start = ((bf16[8,112,128]{2,1,0:T(8,128)(2,1)}), bf16[8,112,128]{2,1,0:T(8,128)(2,1)S(1)}, u32[]{:S(2)}, u32[]{:S(2)}) async-start(bf16[8,112,128]{2,1,0:T(8,128)(2,1)} %shard_map.76), calls=%async_computation | async-start | bytes 458752 | tf_op jit(solution)/shard_map/all_to_all | solution.py:38
  11.9 0.0 copy-start.1
  11.9 0.7 copy-done.1
  12.5 0.0 copy-start.2
  12.5 0.7 copy-done.2
  13.2 10.3 %all-to-all-done = bf16[8,112,128]{2,1,0:T(8,128)(2,1)S(1)} async-done(((bf16[8,112,128]{2,1,0:T(8,128)(2,1)}), bf16[8,112,128]{2,1,0:T(8,128)(2,1)S(1)}, u32[]{:S(2)}, u32[]{:S(2)}) %all-to-all-start) | async-done | bytes 229408 | tf_op jit(solution)/shard_map/all_to_all | solution.py:38
  23.5 2.8 %collective-permute-start.8 = (bf16[448,128]{1,0:T(8,128)(2,1)S(1)}, bf16[448,128]{1,0:T(8,128)(2,1)S(1)}, u32[]{:S(2)}, u32[]{:S(2)}) collective-permute-start(bf16[448,128]{1,0:T(8,128)(2,1)S(1)} %bitcast.44), channel_id=1, source_target_pairs={{64,0},{128,64},{192,128},{0,192},{65,1},{129,65},{193,129},{1,193... | collective-permute-start | bytes 344072 | tf_op jit(solution)/shard_map/ppermute | solution.py:22
  26.3 0.0 collective-permute-start.9
  26.3 1.6 %collective-permute-start.10 = (bf16[448,128]{1,0:T(8,128)(2,1)S(1)}, bf16[448,128]{1,0:T(8,128)(2,1)S(1)}, u32[]{:S(2)}, u32[]{:S(2)}) collective-permute-start(bf16[448,128]{1,0:T(8,128)(2,1)S(1)} %bitcast.46), channel_id=1, source_target_pairs={{128,0},{192,64},{0,128},{64,192},{129,1},{193,65},{1,129},{65,193... | collective-permute-start | bytes 344072 | tf_op jit(solution)/shard_map/ppermute | solution.py:22
  27.9 2.8 %collective-permute-start.2 = (bf16[464,128]{1,0:T(8,128)(2,1)S(1)}, bf16[464,128]{1,0:T(8,128)(2,1)S(1)}, u32[]{:S(2)}, u32[]{:S(2)}) collective-permute-start(bf16[464,128]{1,0:T(8,128)(2,1)S(1)} %pad_maximum_fusion.2), channel_id=1, source_target_pairs={{4,0},{6,2},{0,4},{2,6},{5,1},{7,3},{1,5},{3,7},{12,8},{14,10},{8,... | collective-permute-start | bytes 356360 | tf_op jit(solution)/shard_map/ppermute | solution.py:22
  30.8 0.0 collective-permute-done.8
  30.8 0.3 collective-permute-start.1
  31.1 3.2 %collective-permute-done.9 = bf16[448,128]{1,0:T(8,128)(2,1)S(1)} collective-permute-done((bf16[448,128]{1,0:T(8,128)(2,1)S(1)}, bf16[448,128]{1,0:T(8,128)(2,1)S(1)}, u32[]{:S(2)}, u32[]{:S(2)}) %collective-permute-start.9) | collective-permute-done | bytes 114720 | tf_op jit(solution)/shard_map/ppermute | solution.py:22
  34.3 2.5 %collective-permute-start = (bf16[464,128]{1,0:T(8,128)(2,1)S(1)}, bf16[464,128]{1,0:T(8,128)(2,1)S(1)}, u32[]{:S(2)}, u32[]{:S(2)}) collective-permute-start(bf16[464,128]{1,0:T(8,128)(2,1)S(1)} %pad_maximum_fusion.2), channel_id=1, source_target_pairs={{2,0},{4,2},{6,4},{0,6},{3,1},{5,3},{7,5},{1,7},{10,8},{12,10},{14... | collective-permute-start | bytes 356360 | tf_op jit(solution)/shard_map/ppermute | solution.py:22
  36.8 0.0 collective-permute-done.10
  36.8 0.1 pad_maximum_fusion.1.x0
  36.9 0.6 collective-permute-start.11
  37.5 0.0 collective-permute-done.2
  37.5 0.9 collective-permute-start.12
  38.4 0.0 collective-permute-done.1
  38.5 0.2 collective-permute-done
  38.7 0.1 pad_maximum_fusion.y0
  38.7 0.1 collective-permute-start.3
  38.8 1.5 %collective-permute-start.4 = (bf16[4,448,128]{2,1,0:T(8,128)(2,1)S(1)}, bf16[4,448,128]{2,1,0:T(8,128)(2,1)S(1)}, u32[]{:S(2)}, u32[]{:S(2)}) collective-permute-start(bf16[4,448,128]{2,1,0:T(8,128)(2,1)S(1)} %pad_maximum_fusion.y0), channel_id=1, source_target_pairs={{192,0},{0,64},{64,128},{128,192},{193,1},{1,65},{65,129},{129,193... | collective-permute-start | bytes 1376264 | tf_op jit(solution)/shard_map/ppermute | solution.py:22
  40.3 0.1 stack.86.place
  40.4 7.8 %collective-permute-done.11.x1 = bf16[4,448,128]{2,1,0:T(8,128)(2,1)S(1)} collective-permute-done((bf16[4,448,128]{2,1,0:T(8,128)(2,1)S(1)}, bf16[4,448,128]{2,1,0:T(8,128)(2,1)S(1)}, u32[]{:S(2)}, u32[]{:S(2)}) %collective-permute-start.11) | collective-permute-done | bytes 458784 | tf_op jit(solution)/shard_map/ppermute | solution.py:22
  48.2 3.4 %collective-permute-start.13 = (bf16[2,448,128]{2,1,0:T(8,128)(2,1)S(1)}, bf16[2,448,128]{2,1,0:T(8,128)(2,1)S(1)}, u32[]{:S(2)}, u32[]{:S(2)}) collective-permute-start(bf16[2,448,128]{2,1,0:T(8,128)(2,1)S(1)} %slice.58), channel_id=1, source_target_pairs={{2,0},{4,2},{6,4},{0,6},{3,1},{5,3},{7,5},{1,7},{10,8},{12,10},{14... | collective-permute-start | bytes 688136 | tf_op jit(solution)/shard_map/ppermute | solution.py:22
  51.6 0.0 collective-permute-done.12.x2
  51.6 0.1 collective-permute-start.14
  51.7 0.0 collective-permute-done.3.y1
  51.7 0.1 collective-permute-start.5
  51.8 0.0 collective-permute-done.4.y2
  51.8 1.7 %collective-permute-start.6 = (bf16[2,448,128]{2,1,0:T(8,128)(2,1)S(1)}, bf16[2,448,128]{2,1,0:T(8,128)(2,1)S(1)}, u32[]{:S(2)}, u32[]{:S(2)}) collective-permute-start(bf16[2,448,128]{2,1,0:T(8,128)(2,1)S(1)} %slice.56), channel_id=1, source_target_pairs={{192,0},{0,64},{64,128},{128,192},{193,1},{1,65},{65,129},{129,193... | collective-permute-start | bytes 688136 | tf_op jit(solution)/shard_map/ppermute | solution.py:22
  53.5 0.0 collective-permute-done.7.second
  53.6 5.2 %shard_map.77.held = bf16[2,1000,3584]{2,1,0:T(8,128)(2,1)S(1)} custom-call(bf16[1000,3584]{1,0:T(8,128)(2,1)} %first.1, bf16[1000,3584]{1,0:T(8,128)(2,1)} %collective-permute-done.7.second), custom_call_target="tpu_custom_call" | custom-call | tf_op jit(solution)/shard_map/pallas_call | solution.py:207
  58.8 2.8 %shard_map.78.near = f32[2,1000,256]{2,1,0:T(8,128)S(1)} custom-call(s32[11]{0:T(128)S(1)} %stack.86.place, bf16[4,448,128]{2,1,0:T(8,128)(2,1)S(1)} %pad_maximum_fusion.1.x0, bf16[4,448,128]{2,1,0:T(8,128)(2,1)S(1)} %collective-permute-done.11.x1, bf16[2,1000,3584]{2,1,0:T(8,128)(2,1)S(1)} %shard_map.77.held), custom_call_target="tpu_custom_call" | custom-call | tf_op jit(solution)/shard_map/pallas_call | solution.py:207
  61.5 0.0 collective-permute-done.13.x3
  61.6 0.0 collective-permute-done.14.x4
  61.6 2.8 %shard_map.79.far = f32[2,1000,256]{2,1,0:T(8,128)S(1)} custom-call(s32[11]{0:T(128)S(1)} %stack.86.place, bf16[4,448,128]{2,1,0:T(8,128)(2,1)S(1)} %collective-permute-done.12.x2, bf16[2,448,128]{2,1,0:T(8,128)(2,1)S(1)} %collective-permute-done.13.x3, bf16[2,448,128]{2,1,0:T(8,128)(2,1)S(1)} %collective-permute-done.14.x4, ...), custom_call_target="tpu_custom_call" | custom-call | tf_op jit(solution)/shard_map/pallas_call | solution.py:207
  64.3 0.0 collective-permute-done.5.y3
  64.4 0.0 collective-permute-done.6.y4
  64.4 5.8 %shard_map.80 = f32[16,8,128]{2,1,0:T(8,128)S(1)} custom-call(s32[11]{0:T(128)S(1)} %stack.86.place, bf16[4,16,128]{2,1,0:T(8,128)(2,1)S(1)} %pad_maximum_fusion.3.ints, bf16[4,448,128]{2,1,0:T(8,128)(2,1)S(1)} %pad_maximum_fusion.y0, bf16[4,448,128]{2,1,0:T(8,128)(2,1)S(1)} %collective-permute-done.3.y1, ...), custom_call_target="tpu_custom_call" | custom-call | tf_op jit(solution)/shard_map/pallas_call | solution.py:207
  70.1 11.3 %all_to_all.15.parts = f32[16,8,128]{2,1,0:T(8,128)S(1)} all-to-all(f32[16,8,128]{2,1,0:T(8,128)S(1)} %shard_map.80), channel_id=1, replica_groups=mesh['y'=4,'z'=8,'x'=4,'c'=2] {'y','x'}, dimensions={0} | all-to-all | bytes 131072 | tf_op jit(solution)/shard_map/all_to_all | solution.py:38
  81.5 14.5 %all_to_all.16.parts = f32[16,8,128]{2,1,0:T(8,128)S(1)} all-to-all(f32[16,8,128]{2,1,0:T(8,128)S(1)} %shard_map.81), channel_id=1, replica_groups=mesh['y'=4,'z'=8,'x'=4,'c'=2] {'z','c'}, dimensions={0} | all-to-all | bytes 131072 | tf_op jit(solution)/shard_map/all_to_all | solution.py:38
  96.0 1.2 %shard_map.82 = (f32[1,128]{1,0:T(1,128)}, f32[1,128]{1,0:T(1,128)}, f32[1,1]{1,0:T(1,128)}, f32[1,1]{1,0:T(1,128)}) custom-call(s32[11]{0:T(128)S(1)} %stack.86.place, f32[16,8,128]{2,1,0:T(8,128)S(1)} %all_to_all.16.parts), custom_call_target="tpu_custom_call" | custom-call | tf_op jit(solution)/shard_map/pallas_call | solution.py:207
  (15 shorter events, 0.2 us)
Async XLA Ops:
  0.6 52.9 %collective-permute-start.7 = (bf16[1000,3584]{1,0:T(8,128)(2,1)}, bf16[1000,3584]{1,0:T(8,128)(2,1)}, u32[]{:S(2)}, u32[]{:S(2)}) collective-permute-start(bf16[1000,3584]{1,0:T(8,128)(2,1)} %first.1), channel_id=1, source_target_pairs={{0,1},{1,0},{2,3},{3,2},{4,5},{5,4},{6,7},{7,6},{8,9},{9,8},{10,11... | collective-permute-start | bytes 21504008 | tf_op jit(solution)/shard_map/ppermute | solution.py:221
  3.9 0.7 copy-start
  5.4 18.1 %all-to-all-start = ((bf16[8,112,128]{2,1,0:T(8,128)(2,1)}), bf16[8,112,128]{2,1,0:T(8,128)(2,1)S(1)}, u32[]{:S(2)}, u32[]{:S(2)}) async-start(bf16[8,112,128]{2,1,0:T(8,128)(2,1)} %shard_map.76), calls=%async_computation | async-start | bytes 458752 | tf_op jit(solution)/shard_map/all_to_all | solution.py:38
  11.9 0.7 copy-start.1
  12.5 0.7 copy-start.2
  23.5 7.3 %collective-permute-start.8 = (bf16[448,128]{1,0:T(8,128)(2,1)S(1)}, bf16[448,128]{1,0:T(8,128)(2,1)S(1)}, u32[]{:S(2)}, u32[]{:S(2)}) collective-permute-start(bf16[448,128]{1,0:T(8,128)(2,1)S(1)} %bitcast.44), channel_id=1, source_target_pairs={{64,0},{128,64},{192,128},{0,192},{65,1},{129,65},{193,129},{1,193... | collective-permute-start | bytes 344072 | tf_op jit(solution)/shard_map/ppermute | solution.py:22
  26.3 8.0 %collective-permute-start.9 = (bf16[448,128]{1,0:T(8,128)(2,1)S(1)}, bf16[448,128]{1,0:T(8,128)(2,1)S(1)}, u32[]{:S(2)}, u32[]{:S(2)}) collective-permute-start(bf16[448,128]{1,0:T(8,128)(2,1)S(1)} %bitcast.45), channel_id=1, source_target_pairs={{192,0},{0,64},{64,128},{128,192},{193,1},{1,65},{65,129},{129,193... | collective-permute-start | bytes 344072 | tf_op jit(solution)/shard_map/ppermute | solution.py:22
  26.3 10.5 %collective-permute-start.10 = (bf16[448,128]{1,0:T(8,128)(2,1)S(1)}, bf16[448,128]{1,0:T(8,128)(2,1)S(1)}, u32[]{:S(2)}, u32[]{:S(2)}) collective-permute-start(bf16[448,128]{1,0:T(8,128)(2,1)S(1)} %bitcast.46), channel_id=1, source_target_pairs={{128,0},{192,64},{0,128},{64,192},{129,1},{193,65},{1,129},{65,193... | collective-permute-start | bytes 344072 | tf_op jit(solution)/shard_map/ppermute | solution.py:22
  27.9 9.6 %collective-permute-start.2 = (bf16[464,128]{1,0:T(8,128)(2,1)S(1)}, bf16[464,128]{1,0:T(8,128)(2,1)S(1)}, u32[]{:S(2)}, u32[]{:S(2)}) collective-permute-start(bf16[464,128]{1,0:T(8,128)(2,1)S(1)} %pad_maximum_fusion.2), channel_id=1, source_target_pairs={{4,0},{6,2},{0,4},{2,6},{5,1},{7,3},{1,5},{3,7},{12,8},{14,10},{8,... | collective-permute-start | bytes 356360 | tf_op jit(solution)/shard_map/ppermute | solution.py:22
  30.8 7.7 %collective-permute-start.1 = (bf16[464,128]{1,0:T(8,128)(2,1)S(1)}, bf16[464,128]{1,0:T(8,128)(2,1)S(1)}, u32[]{:S(2)}, u32[]{:S(2)}) collective-permute-start(bf16[464,128]{1,0:T(8,128)(2,1)S(1)} %pad_maximum_fusion.2), channel_id=1, source_target_pairs={{6,0},{0,2},{2,4},{4,6},{7,1},{1,3},{3,5},{5,7},{14,8},{8,10},{10,... | collective-permute-start | bytes 356360 | tf_op jit(solution)/shard_map/ppermute | solution.py:22
  34.3 4.3 %collective-permute-start = (bf16[464,128]{1,0:T(8,128)(2,1)S(1)}, bf16[464,128]{1,0:T(8,128)(2,1)S(1)}, u32[]{:S(2)}, u32[]{:S(2)}) collective-permute-start(bf16[464,128]{1,0:T(8,128)(2,1)S(1)} %pad_maximum_fusion.2), channel_id=1, source_target_pairs={{2,0},{4,2},{6,4},{0,6},{3,1},{5,3},{7,5},{1,7},{10,8},{12,10},{14... | collective-permute-start | bytes 356360 | tf_op jit(solution)/shard_map/ppermute | solution.py:22
  36.9 11.3 %collective-permute-start.11 = (bf16[4,448,128]{2,1,0:T(8,128)(2,1)S(1)}, bf16[4,448,128]{2,1,0:T(8,128)(2,1)S(1)}, u32[]{:S(2)}, u32[]{:S(2)}) collective-permute-start(bf16[4,448,128]{2,1,0:T(8,128)(2,1)S(1)} %pad_maximum_fusion.1.x0), channel_id=1, source_target_pairs={{2,0},{4,2},{6,4},{0,6},{3,1},{5,3},{7,5},{1,7},{10,8},{12,10},{14... | collective-permute-start | bytes 1376264 | tf_op jit(solution)/shard_map/ppermute | solution.py:22
  37.5 14.1 %collective-permute-start.12 = (bf16[4,448,128]{2,1,0:T(8,128)(2,1)S(1)}, bf16[4,448,128]{2,1,0:T(8,128)(2,1)S(1)}, u32[]{:S(2)}, u32[]{:S(2)}) collective-permute-start(bf16[4,448,128]{2,1,0:T(8,128)(2,1)S(1)} %pad_maximum_fusion.1.x0), channel_id=1, source_target_pairs={{6,0},{0,2},{2,4},{4,6},{7,1},{1,3},{3,5},{5,7},{14,8},{8,10},{10,... | collective-permute-start | bytes 1376264 | tf_op jit(solution)/shard_map/ppermute | solution.py:22
  38.7 12.9 %collective-permute-start.3 = (bf16[4,448,128]{2,1,0:T(8,128)(2,1)S(1)}, bf16[4,448,128]{2,1,0:T(8,128)(2,1)S(1)}, u32[]{:S(2)}, u32[]{:S(2)}) collective-permute-start(bf16[4,448,128]{2,1,0:T(8,128)(2,1)S(1)} %pad_maximum_fusion.y0), channel_id=1, source_target_pairs={{64,0},{128,64},{192,128},{0,192},{65,1},{129,65},{193,129},{1,193... | collective-permute-start | bytes 1376264 | tf_op jit(solution)/shard_map/ppermute | solution.py:22
  38.8 13.0 %collective-permute-start.4 = (bf16[4,448,128]{2,1,0:T(8,128)(2,1)S(1)}, bf16[4,448,128]{2,1,0:T(8,128)(2,1)S(1)}, u32[]{:S(2)}, u32[]{:S(2)}) collective-permute-start(bf16[4,448,128]{2,1,0:T(8,128)(2,1)S(1)} %pad_maximum_fusion.y0), channel_id=1, source_target_pairs={{192,0},{0,64},{64,128},{128,192},{193,1},{1,65},{65,129},{129,193... | collective-permute-start | bytes 1376264 | tf_op jit(solution)/shard_map/ppermute | solution.py:22
  48.2 13.4 %collective-permute-start.13 = (bf16[2,448,128]{2,1,0:T(8,128)(2,1)S(1)}, bf16[2,448,128]{2,1,0:T(8,128)(2,1)S(1)}, u32[]{:S(2)}, u32[]{:S(2)}) collective-permute-start(bf16[2,448,128]{2,1,0:T(8,128)(2,1)S(1)} %slice.58), channel_id=1, source_target_pairs={{2,0},{4,2},{6,4},{0,6},{3,1},{5,3},{7,5},{1,7},{10,8},{12,10},{14... | collective-permute-start | bytes 688136 | tf_op jit(solution)/shard_map/ppermute | solution.py:22
  51.6 10.0 %collective-permute-start.14 = (bf16[2,448,128]{2,1,0:T(8,128)(2,1)S(1)}, bf16[2,448,128]{2,1,0:T(8,128)(2,1)S(1)}, u32[]{:S(2)}, u32[]{:S(2)}) collective-permute-start(bf16[2,448,128]{2,1,0:T(8,128)(2,1)S(1)} %slice.59), channel_id=1, source_target_pairs={{6,0},{0,2},{2,4},{4,6},{7,1},{1,3},{3,5},{5,7},{14,8},{8,10},{10,... | collective-permute-start | bytes 688136 | tf_op jit(solution)/shard_map/ppermute | solution.py:22
  51.7 12.6 %collective-permute-start.5 = (bf16[2,448,128]{2,1,0:T(8,128)(2,1)S(1)}, bf16[2,448,128]{2,1,0:T(8,128)(2,1)S(1)}, u32[]{:S(2)}, u32[]{:S(2)}) collective-permute-start(bf16[2,448,128]{2,1,0:T(8,128)(2,1)S(1)} %slice.55), channel_id=1, source_target_pairs={{64,0},{128,64},{192,128},{0,192},{65,1},{129,65},{193,129},{1,193... | collective-permute-start | bytes 688136 | tf_op jit(solution)/shard_map/ppermute | solution.py:22
  51.8 12.5 %collective-permute-start.6 = (bf16[2,448,128]{2,1,0:T(8,128)(2,1)S(1)}, bf16[2,448,128]{2,1,0:T(8,128)(2,1)S(1)}, u32[]{:S(2)}, u32[]{:S(2)}) collective-permute-start(bf16[2,448,128]{2,1,0:T(8,128)(2,1)S(1)} %slice.56), channel_id=1, source_target_pairs={{192,0},{0,64},{64,128},{128,192},{193,1},{1,65},{65,129},{129,193... | collective-permute-start | bytes 688136 | tf_op jit(solution)/shard_map/ppermute | solution.py:22
